TPU v7x, 128 devices: a whole 4x4x4 slice. The times are simulated.
128 devices in a mesh: slab: 32 (over z, y, core), plane: 4 (over x).
Axes of the slice: x: 4, y: 4, z: 4, core: 2. Of those that a mesh axis runs over, the one named last changes fastest.
Arguments:
- tissue_v: float32 [128, 64, 128], P('slab', 'plane'), may hold values from -4 to 4
- tissue_gates: float32 [40, 128, 64, 128], P(None, 'slab', 'plane'), may hold values from 0 to 1
- tissue_diff: float32 [128, 64, 128], P('slab', 'plane'), may hold values from 0.2 to 1
- fibre_v: float32 [512, 2048], P('slab', 'plane'), may hold values from -4 to 4
- fibre_gates: float32 [40, 512, 2048], P(None, 'slab', 'plane'), may hold values from 0 to 1
- fibre_diff: float32 [512, 2048], P('slab', 'plane'), may hold values from 0.2 to 1
- gate_half: float32 [40], replicated, may hold values from -3 to 3
- gate_rate: float32 [40], replicated, may hold values from 0.5 to 20
- gate_cond: float32 [40], replicated, may hold values from 0.01 to 0.15
- gate_rev: float32 [40], replicated, may hold values from -2 to 2
- junc_cond: float32 [8], replicated, may hold values from 0.25 to 2
- junc_fibre: int32 [524288], P(('slab', 'plane')), may hold values from 0 to 15
- junc_fcell: int32 [524288], P(('slab', 'plane')), may hold values from 0 to 511
- junc_owner: int32 [524288, 1], P(('slab', 'plane')), may hold values from 0 to 127; in each aligned block of 4096 rows (0 to 4095, 4096 to 8191, ...) at most 64 rows name the same one
- junc_tcell: int32 [524288], P(('slab', 'plane')), may hold values from 0 to 8191
- junc_class: int32 [524288], P(('slab', 'plane')), may hold values from 0 to 7
Outputs:
- tissue_out: float32 [128, 64, 128], P('slab', 'plane')
- fibre_out: float32 [512, 2048], P('slab', 'plane')
Inputs may be any that keep to these rules, and one draw needn't show every extreme that they name: `junc_owner`: among the junctions held by one device, no tissue block is named by more than 64 of them, and some block is named by exactly 64. `junc_fibre`: A fibre of the slab group of the device that holds the junction. `junc_fcell`: A cell of the holding device's share of that fibre. `junc_tcell`: numbered over the owner's block in the order z, y, x with x fastest.
All inputs are finite; a program needn't handle non-finite values.
Results may differ from a plain program's by a relative error of at most 0.00005.
Values sent between devices are 32-bit elements; how exact they have to be, the bound alone decides.
No kernel may reach another device: no remote copies, remote signals or barrier semaphores. Data moves between devices by JAX's collectives and lax.ppermute only.
A program may use at most 64 MiB of HBM per device.

v0:
```python
import jax
import jax.numpy as jnp
from jax import lax
from jax.sharding import PartitionSpec as P

STEPS = 14


time_step = 0.1
gate_slope = 2.0


def extended(array, sides, width):
    edges = {}
    for axis, dim in sides:
        peers, length = (lax.axis_size(axis), array.shape[dim])
        up = [(i, (i + 1) % peers) for i in range(peers - 1)]
        last = lax.slice_in_dim(array, length - width, length, axis=dim)
        first = lax.slice_in_dim(array, 0, width, axis=dim)
        edges[dim] = (
            lax.ppermute(last, axis, up),
            lax.ppermute(first, axis, [(b, a) for a, b in up]),
        )
    done = []
    for _, dim in sides:
        low, high = edges[dim]
        around = [(width, width) if d in done else (0, 0) for d in range(array.ndim)]
        array = jnp.concatenate([jnp.pad(low, around), array, jnp.pad(high, around)], axis=dim)
        done.append(dim)
    return array


def with_halo(block, sides, width):
    for axis, dim in sides:
        count = lax.axis_size(axis)
        forward = [(i, i + 1) for i in range(count - 1)]
        backward = [(target, source) for source, target in forward]
        low = lax.ppermute(
            lax.slice_in_dim(block, block.shape[dim] - width, None, axis=dim), axis, forward
        )
        high = lax.ppermute(lax.slice_in_dim(block, 0, width, axis=dim), axis, backward)
        block = jnp.concatenate([low, block, high], axis=dim)
    return block


def membrane(voltage, gates, gate_half, gate_rate, gate_cond, gate_rev):
    gate_shape = (gates.shape[0],) + (1,) * (gates.ndim - 1)
    gate_signs = (
        jnp.where(jnp.arange(gates.shape[0], dtype=jnp.int32) % 2 == 0, 1.0, -1.0)
        .astype(jnp.float32)
        .reshape(gate_shape)
    )
    shifted = voltage[None] - gate_half.reshape(gate_shape)
    steady = jax.nn.sigmoid(gate_signs * gate_slope * shifted)
    decay_factor = jnp.exp(
        -time_step * gate_rate.reshape(gate_shape) * (1.0 + jax.nn.sigmoid(shifted))
    )
    renewed = steady + (gates - steady) * decay_factor
    conduct = jnp.tensordot(gate_cond, renewed, axes=1, precision=lax.Precision.HIGHEST)
    driven = jnp.tensordot(gate_cond * gate_rev, renewed, axes=1, precision=lax.Precision.HIGHEST)
    return (renewed, voltage * conduct - driven)


def line_count(length, offset, total):
    places = offset + jnp.arange(length, dtype=jnp.int32)
    return (places > 0).astype(jnp.float32) + (places < total - 1).astype(jnp.float32)


def class_gain(classes, junc_cond):
    return jnp.sum(
        jnp.where(
            classes[:, None] == jnp.arange(junc_cond.shape[0], dtype=jnp.int32)[None, :],
            junc_cond[None, :],
            jnp.zeros((), jnp.float32),
        ),
        axis=1,
    )


def make_onehot(indices, count):
    return (indices[:, None] == jnp.arange(count, dtype=jnp.int32)[None, :]).astype(jnp.float32)


def pick_values(row_onehot, col_onehot, table):
    rows_read = jnp.dot(
        row_onehot, table, precision=lax.Precision.HIGHEST, preferred_element_type=jnp.float32
    )
    return jnp.sum(rows_read * col_onehot, axis=1)


def place_values(row_onehot, col_onehot, values):
    weighted = col_onehot * values[:, None]
    return lax.dot_general(
        row_onehot,
        weighted,
        (((0,), (0,)), ((), ())),
        precision=lax.Precision.HIGHEST,
        preferred_element_type=jnp.float32,
    )


def trade_both(paired):
    return lax.all_to_all(paired, ("slab", "plane"), split_axis=1, concat_axis=1, tiled=True)


def body(
    tissue_v,
    tissue_gates,
    tissue_diff,
    fibre_v,
    fibre_gates,
    fibre_diff,
    gate_half,
    gate_rate,
    gate_cond,
    gate_rev,
    junc_cond,
    junc_fibre,
    junc_fcell,
    junc_owner,
    junc_tcell,
    junc_class,
):
    slab_count = lax.axis_size("slab")
    plane_count = lax.axis_size("plane")
    devices = slab_count * plane_count
    layers_dev, rows_dev, cols_dev = tissue_v.shape
    fibre_rows, fibre_cols = fibre_v.shape
    junctions = junc_fibre.shape[0]
    capacity = 2 * junctions // devices
    tissue_count = (
        line_count(layers_dev, lax.axis_index("slab") * layers_dev, layers_dev * slab_count)[
            :, None, None
        ]
        + line_count(rows_dev, lax.axis_index("plane") * rows_dev, rows_dev * plane_count)[
            None, :, None
        ]
        + line_count(cols_dev, 0, cols_dev)[None, None, :]
    )
    fibre_count = line_count(
        fibre_cols, lax.axis_index("plane") * fibre_cols, fibre_cols * plane_count
    )[None, :]
    fibre_cells = fibre_rows * fibre_cols
    fibre_width = 128
    fibre_grid_rows = fibre_cells // fibre_width
    tissue_grid_rows = layers_dev * rows_dev
    owners = junc_owner[:, 0]
    owner_onehot = make_onehot(owners, devices)
    owner_table = owner_onehot.astype(jnp.int32)
    slot_rank = jnp.sum(jnp.cumsum(owner_table, axis=0) * owner_table, axis=1) - 1
    rank_onehot = make_onehot(slot_rank, capacity)
    slot_index = owners * capacity + slot_rank
    fibre_index = junc_fibre * fibre_cols + junc_fcell
    fibre_row_onehot = make_onehot(fibre_index // fibre_width, fibre_grid_rows)
    fibre_col_onehot = make_onehot(fibre_index % fibre_width, fibre_width)
    cell_table = jnp.zeros((devices * capacity,), jnp.int32).at[slot_index].set(junc_tcell)
    class_table = jnp.full((devices * capacity,), -1, jnp.int32).at[slot_index].set(junc_class)
    sent_tables = jnp.stack([cell_table, class_table]).reshape(2, devices, capacity)
    got_tables = lax.all_to_all(
        sent_tables, ("slab", "plane"), split_axis=1, concat_axis=1, tiled=True
    )
    remote_cells = got_tables[0].reshape(-1)
    remote_gain = class_gain(got_tables[1].reshape(-1), junc_cond)
    own_gain = class_gain(junc_class, junc_cond)
    cell_row_onehot = make_onehot(remote_cells // cols_dev, tissue_grid_rows)
    cell_col_onehot = make_onehot(remote_cells % cols_dev, cols_dev)

    def advance(step_index, carry):
        tissue_now, tissue_state, fibre_now, fibre_state = carry
        fibre_grid = fibre_now.reshape(fibre_grid_rows, fibre_width)
        tissue_grid = tissue_now.reshape(tissue_grid_rows, cols_dev)
        fibre_at_junction = pick_values(fibre_row_onehot, fibre_col_onehot, fibre_grid)
        outgoing = place_values(owner_onehot, rank_onehot, fibre_at_junction)
        tissue_at_slot = pick_values(cell_row_onehot, cell_col_onehot, tissue_grid)
        paired = jnp.stack([outgoing, tissue_at_slot.reshape(devices, capacity)])
        traded = trade_both(paired)
        current = remote_gain * (traded[0].reshape(-1) - tissue_at_slot)
        fibre_current = own_gain * (
            fibre_at_junction - pick_values(owner_onehot, rank_onehot, traded[1])
        )
        tissue_source = place_values(cell_row_onehot, cell_col_onehot, current).reshape(
            tissue_now.shape
        )
        fibre_source = place_values(fibre_row_onehot, fibre_col_onehot, fibre_current).reshape(
            fibre_now.shape
        )
        padded = extended(tissue_now, (("slab", 0), ("plane", 1)), 1)
        sides = jnp.pad(tissue_now, ((0, 0), (0, 0), (1, 1)))
        neighbours = (
            padded[2:, 1:-1]
            + padded[:-2, 1:-1]
            + padded[1:-1, 2:]
            + padded[1:-1, :-2]
            + sides[:, :, 2:]
            + sides[:, :, :-2]
        )
        tissue_lap = neighbours - tissue_count * tissue_now
        fibre_padded = with_halo(fibre_now, (("plane", 1),), 1)
        fibre_lap = fibre_padded[:, 2:] + fibre_padded[:, :-2] - fibre_count * fibre_now
        tissue_state, tissue_ionic = membrane(
            tissue_now, tissue_state, gate_half, gate_rate, gate_cond, gate_rev
        )
        fibre_state, fibre_ionic = membrane(
            fibre_now, fibre_state, gate_half, gate_rate, gate_cond, gate_rev
        )
        tissue_next = tissue_now + time_step * (
            tissue_diff * tissue_lap - tissue_ionic + tissue_source
        )
        fibre_next = fibre_now + time_step * (fibre_diff * fibre_lap - fibre_ionic - fibre_source)
        return (tissue_next, tissue_state, fibre_next, fibre_state)

    final = lax.fori_loop(0, STEPS, advance, (tissue_v, tissue_gates, fibre_v, fibre_gates))
    return (final[0], final[2])


def solution(mesh):
    in_specs = (
        P("slab", "plane", None),
        P(None, "slab", "plane", None),
        P("slab", "plane", None),
        P("slab", "plane"),
        P(None, "slab", "plane"),
        P("slab", "plane"),
        P(),
        P(),
        P(),
        P(),
        P(),
        P(("slab", "plane")),
        P(("slab", "plane")),
        P(("slab", "plane"), None),
        P(("slab", "plane")),
        P(("slab", "plane")),
    )
    out_specs = (P("slab", "plane", None), P("slab", "plane"))
    return jax.shard_map(body, mesh=mesh, in_specs=in_specs, out_specs=out_specs, check_vma=False)
```

profile of v0, /device:TPU:34, one launch (start us, length us, event | category | flops | bytes accessed | tf_op | source)
XLA Modules:
  0.0 872.6 jit_solution(15111886859840716385)
XLA Ops:
  5.3 15.9 %scatter_custom_fusion = s32[8192]{0:T(1024)S(1)} fusion(s32[4096]{0:T(1024)S(1)} %bitcast.121, s32[4096]{0:T(1024)} %param.32, s32[]{:T(128)} %copy.102), kind=kCustom, calls=%fused_computation.175 | custom fusion | bytes 33280 | tf_op jit(solution)/shard_map/scatter | solution.py:156
  21.2 15.5 %scatter_custom_fusion.1 = s32[8192]{0:T(1024)S(1)} fusion(s32[4096]{0:T(1024)S(1)} %bitcast.122, s32[4096]{0:T(1024)S(1)} %copy-done.11, s32[]{:T(128)} %constant.147.clone.1), kind=kCustom, calls=%fused_computation.173 | custom fusion | bytes 32772 | tf_op jit(solution)/shard_map/scatter | solution.py:157
  38.0 10.2 %all-to-all-start.1 = ((s32[128,1,128]{2,1,0:T(1,128)}), s32[128,1,128]{2,1,0:T(1,128)S(1)}, u32[]{:S(2)}, u32[]{:S(2)}) async-start(s32[128,1,128]{2,1,0:T(1,128)} %reshape.328), calls=%async_computation.1 | async-start | bytes 131072 | tf_op jit(solution)/shard_map/all_to_all | solution.py:159
  48.2 7.9 all-to-all-done.1
  58.3 813.6 %while.19 = (s32[]{:T(128)}, f32[4,16,128]{2,1,0:T(8,128)S(1)}, f32[40,4,16,128]{3,2,1,0:T(8,128)S(1)}, f32[16,512]{1,0:T(8,128)S(1)}, f32[40,16,512]{2,1,0:T(8,...) while((s32[]{:T(128)}, f32[4,16,128]{2,1,0:T(8,128)S(1)}, ...), condition=%wide.region_11.12_spmd.clone, body=%wide.region_7.11_spmd.clone.sunk | while | flops 3260222976 | bytes 13602965 | solution.py:212
  68.1 6.1 all-to-all-start
  76.3 5.6 collective-permute-start.1
  124.8 7.7 all-to-all-start
  134.5 5.6 collective-permute-start.1
  183.0 7.7 all-to-all-start
  192.7 5.6 collective-permute-start.1
  241.2 7.7 all-to-all-start
  250.9 5.6 collective-permute-start.1
  299.4 7.7 all-to-all-start
  309.1 5.6 collective-permute-start.1
  357.6 7.7 all-to-all-start
  415.9 7.7 all-to-all-start
  474.1 7.7 all-to-all-start
  532.3 7.7 all-to-all-start
  590.5 7.7 all-to-all-start
  648.7 7.7 all-to-all-start
  706.9 7.7 all-to-all-start
  765.1 7.7 all-to-all-start
  823.4 7.7 all-to-all-start
  (772 shorter events, 683.3 us)
Async XLA Ops:
  68.1 34.2 %all-to-all-start = ((f32[128,1,128]{2,1,0:T(1,128)}), f32[128,1,128]{2,1,0:T(1,128)S(1)}, u32[]{:S(2)}, u32[]{:S(2)}) async-start(f32[128,1,128]{2,1,0:T(1,128)} %reshape.337), calls=%async_computation | async-start | bytes 131072 | tf_op jit(solution)/shard_map/while/body/eval_jaxpr/all_to_all | solution.py:103
  81.9 33.1 %collective-permute-start.2 = (f32[4,1,128]{2,1,0:T(1,128)S(1)}, f32[4,1,128]{2,1,0:T(1,128)S(1)}, u32[]{:S(2)}, u32[]{:S(2)}) collective-permute-start(f32[4,1,128]{2,1,0:T(1,128)S(1)} %get-tuple-element.536), channel_id=1, source_target_pairs={{0,1},{1,2},{2,3},{4,5},{5,6},{6,7},{8,9},{9,10},{10,11},{12,13},{... | collective-permute-start | bytes 6152 | tf_op jit(solution)/shard_map/while/body/eval_jaxpr/ppermute | solution.py:21
  124.8 35.8 %all-to-all-start = ((f32[128,1,128]{2,1,0:T(1,128)}), f32[128,1,128]{2,1,0:T(1,128)S(1)}, u32[]{:S(2)}, u32[]{:S(2)}) async-start(f32[128,1,128]{2,1,0:T(1,128)} %reshape.337), calls=%async_computation | async-start | bytes 131072 | tf_op jit(solution)/shard_map/while/body/eval_jaxpr/all_to_all | solution.py:103
  140.2 33.1 %collective-permute-start.2 = (f32[4,1,128]{2,1,0:T(1,128)S(1)}, f32[4,1,128]{2,1,0:T(1,128)S(1)}, u32[]{:S(2)}, u32[]{:S(2)}) collective-permute-start(f32[4,1,128]{2,1,0:T(1,128)S(1)} %get-tuple-element.536), channel_id=1, source_target_pairs={{0,1},{1,2},{2,3},{4,5},{5,6},{6,7},{8,9},{9,10},{10,11},{12,13},{... | collective-permute-start | bytes 6152 | tf_op jit(solution)/shard_map/while/body/eval_jaxpr/ppermute | solution.py:21
  183.0 35.8 %all-to-all-start = ((f32[128,1,128]{2,1,0:T(1,128)}), f32[128,1,128]{2,1,0:T(1,128)S(1)}, u32[]{:S(2)}, u32[]{:S(2)}) async-start(f32[128,1,128]{2,1,0:T(1,128)} %reshape.337), calls=%async_computation | async-start | bytes 131072 | tf_op jit(solution)/shard_map/while/body/eval_jaxpr/all_to_all | solution.py:103
  198.4 33.1 %collective-permute-start.2 = (f32[4,1,128]{2,1,0:T(1,128)S(1)}, f32[4,1,128]{2,1,0:T(1,128)S(1)}, u32[]{:S(2)}, u32[]{:S(2)}) collective-permute-start(f32[4,1,128]{2,1,0:T(1,128)S(1)} %get-tuple-element.536), channel_id=1, source_target_pairs={{0,1},{1,2},{2,3},{4,5},{5,6},{6,7},{8,9},{9,10},{10,11},{12,13},{... | collective-permute-start | bytes 6152 | tf_op jit(solution)/shard_map/while/body/eval_jaxpr/ppermute | solution.py:21
  241.2 35.8 %all-to-all-start = ((f32[128,1,128]{2,1,0:T(1,128)}), f32[128,1,128]{2,1,0:T(1,128)S(1)}, u32[]{:S(2)}, u32[]{:S(2)}) async-start(f32[128,1,128]{2,1,0:T(1,128)} %reshape.337), calls=%async_computation | async-start | bytes 131072 | tf_op jit(solution)/shard_map/while/body/eval_jaxpr/all_to_all | solution.py:103
  256.6 33.1 %collective-permute-start.2 = (f32[4,1,128]{2,1,0:T(1,128)S(1)}, f32[4,1,128]{2,1,0:T(1,128)S(1)}, u32[]{:S(2)}, u32[]{:S(2)}) collective-permute-start(f32[4,1,128]{2,1,0:T(1,128)S(1)} %get-tuple-element.536), channel_id=1, source_target_pairs={{0,1},{1,2},{2,3},{4,5},{5,6},{6,7},{8,9},{9,10},{10,11},{12,13},{... | collective-permute-start | bytes 6152 | tf_op jit(solution)/shard_map/while/body/eval_jaxpr/ppermute | solution.py:21
  299.4 35.8 %all-to-all-start = ((f32[128,1,128]{2,1,0:T(1,128)}), f32[128,1,128]{2,1,0:T(1,128)S(1)}, u32[]{:S(2)}, u32[]{:S(2)}) async-start(f32[128,1,128]{2,1,0:T(1,128)} %reshape.337), calls=%async_computation | async-start | bytes 131072 | tf_op jit(solution)/shard_map/while/body/eval_jaxpr/all_to_all | solution.py:103
  314.8 33.1 %collective-permute-start.2 = (f32[4,1,128]{2,1,0:T(1,128)S(1)}, f32[4,1,128]{2,1,0:T(1,128)S(1)}, u32[]{:S(2)}, u32[]{:S(2)}) collective-permute-start(f32[4,1,128]{2,1,0:T(1,128)S(1)} %get-tuple-element.536), channel_id=1, source_target_pairs={{0,1},{1,2},{2,3},{4,5},{5,6},{6,7},{8,9},{9,10},{10,11},{12,13},{... | collective-permute-start | bytes 6152 | tf_op jit(solution)/shard_map/while/body/eval_jaxpr/ppermute | solution.py:21
  357.6 35.8 %all-to-all-start = ((f32[128,1,128]{2,1,0:T(1,128)}), f32[128,1,128]{2,1,0:T(1,128)S(1)}, u32[]{:S(2)}, u32[]{:S(2)}) async-start(f32[128,1,128]{2,1,0:T(1,128)} %reshape.337), calls=%async_computation | async-start | bytes 131072 | tf_op jit(solution)/shard_map/while/body/eval_jaxpr/all_to_all | solution.py:103
  373.0 33.1 %collective-permute-start.2 = (f32[4,1,128]{2,1,0:T(1,128)S(1)}, f32[4,1,128]{2,1,0:T(1,128)S(1)}, u32[]{:S(2)}, u32[]{:S(2)}) collective-permute-start(f32[4,1,128]{2,1,0:T(1,128)S(1)} %get-tuple-element.536), channel_id=1, source_target_pairs={{0,1},{1,2},{2,3},{4,5},{5,6},{6,7},{8,9},{9,10},{10,11},{12,13},{... | collective-permute-start | bytes 6152 | tf_op jit(solution)/shard_map/while/body/eval_jaxpr/ppermute | solution.py:21
  415.9 35.8 %all-to-all-start = ((f32[128,1,128]{2,1,0:T(1,128)}), f32[128,1,128]{2,1,0:T(1,128)S(1)}, u32[]{:S(2)}, u32[]{:S(2)}) async-start(f32[128,1,128]{2,1,0:T(1,128)} %reshape.337), calls=%async_computation | async-start | bytes 131072 | tf_op jit(solution)/shard_map/while/body/eval_jaxpr/all_to_all | solution.py:103
  431.2 33.1 %collective-permute-start.2 = (f32[4,1,128]{2,1,0:T(1,128)S(1)}, f32[4,1,128]{2,1,0:T(1,128)S(1)}, u32[]{:S(2)}, u32[]{:S(2)}) collective-permute-start(f32[4,1,128]{2,1,0:T(1,128)S(1)} %get-tuple-element.536), channel_id=1, source_target_pairs={{0,1},{1,2},{2,3},{4,5},{5,6},{6,7},{8,9},{9,10},{10,11},{12,13},{... | collective-permute-start | bytes 6152 | tf_op jit(solution)/shard_map/while/body/eval_jaxpr/ppermute | solution.py:21
  474.1 35.8 %all-to-all-start = ((f32[128,1,128]{2,1,0:T(1,128)}), f32[128,1,128]{2,1,0:T(1,128)S(1)}, u32[]{:S(2)}, u32[]{:S(2)}) async-start(f32[128,1,128]{2,1,0:T(1,128)} %reshape.337), calls=%async_computation | async-start | bytes 131072 | tf_op jit(solution)/shard_map/while/body/eval_jaxpr/all_to_all | solution.py:103
  489.4 33.1 %collective-permute-start.2 = (f32[4,1,128]{2,1,0:T(1,128)S(1)}, f32[4,1,128]{2,1,0:T(1,128)S(1)}, u32[]{:S(2)}, u32[]{:S(2)}) collective-permute-start(f32[4,1,128]{2,1,0:T(1,128)S(1)} %get-tuple-element.536), channel_id=1, source_target_pairs={{0,1},{1,2},{2,3},{4,5},{5,6},{6,7},{8,9},{9,10},{10,11},{12,13},{... | collective-permute-start | bytes 6152 | tf_op jit(solution)/shard_map/while/body/eval_jaxpr/ppermute | solution.py:21
  532.3 35.8 %all-to-all-start = ((f32[128,1,128]{2,1,0:T(1,128)}), f32[128,1,128]{2,1,0:T(1,128)S(1)}, u32[]{:S(2)}, u32[]{:S(2)}) async-start(f32[128,1,128]{2,1,0:T(1,128)} %reshape.337), calls=%async_computation | async-start | bytes 131072 | tf_op jit(solution)/shard_map/while/body/eval_jaxpr/all_to_all | solution.py:103
  547.7 33.1 %collective-permute-start.2 = (f32[4,1,128]{2,1,0:T(1,128)S(1)}, f32[4,1,128]{2,1,0:T(1,128)S(1)}, u32[]{:S(2)}, u32[]{:S(2)}) collective-permute-start(f32[4,1,128]{2,1,0:T(1,128)S(1)} %get-tuple-element.536), channel_id=1, source_target_pairs={{0,1},{1,2},{2,3},{4,5},{5,6},{6,7},{8,9},{9,10},{10,11},{12,13},{... | collective-permute-start | bytes 6152 | tf_op jit(solution)/shard_map/while/body/eval_jaxpr/ppermute | solution.py:21
  590.5 35.8 %all-to-all-start = ((f32[128,1,128]{2,1,0:T(1,128)}), f32[128,1,128]{2,1,0:T(1,128)S(1)}, u32[]{:S(2)}, u32[]{:S(2)}) async-start(f32[128,1,128]{2,1,0:T(1,128)} %reshape.337), calls=%async_computation | async-start | bytes 131072 | tf_op jit(solution)/shard_map/while/body/eval_jaxpr/all_to_all | solution.py:103
  648.7 35.8 %all-to-all-start = ((f32[128,1,128]{2,1,0:T(1,128)}), f32[128,1,128]{2,1,0:T(1,128)S(1)}, u32[]{:S(2)}, u32[]{:S(2)}) async-start(f32[128,1,128]{2,1,0:T(1,128)} %reshape.337), calls=%async_computation | async-start | bytes 131072 | tf_op jit(solution)/shard_map/while/body/eval_jaxpr/all_to_all | solution.py:103
  706.9 35.8 %all-to-all-start = ((f32[128,1,128]{2,1,0:T(1,128)}), f32[128,1,128]{2,1,0:T(1,128)S(1)}, u32[]{:S(2)}, u32[]{:S(2)}) async-start(f32[128,1,128]{2,1,0:T(1,128)} %reshape.337), calls=%async_computation | async-start | bytes 131072 | tf_op jit(solution)/shard_map/while/body/eval_jaxpr/all_to_all | solution.py:103
  765.1 35.8 %all-to-all-start = ((f32[128,1,128]{2,1,0:T(1,128)}), f32[128,1,128]{2,1,0:T(1,128)S(1)}, u32[]{:S(2)}, u32[]{:S(2)}) async-start(f32[128,1,128]{2,1,0:T(1,128)} %reshape.337), calls=%async_computation | async-start | bytes 131072 | tf_op jit(solution)/shard_map/while/body/eval_jaxpr/all_to_all | solution.py:103
  823.4 35.8 %all-to-all-start = ((f32[128,1,128]{2,1,0:T(1,128)}), f32[128,1,128]{2,1,0:T(1,128)S(1)}, u32[]{:S(2)}, u32[]{:S(2)}) async-start(f32[128,1,128]{2,1,0:T(1,128)} %reshape.337), calls=%async_computation | async-start | bytes 131072 | tf_op jit(solution)/shard_map/while/body/eval_jaxpr/all_to_all | solution.py:103
  838.7 33.1 %collective-permute-start.2 = (f32[4,1,128]{2,1,0:T(1,128)S(1)}, f32[4,1,128]{2,1,0:T(1,128)S(1)}, u32[]{:S(2)}, u32[]{:S(2)}) collective-permute-start(f32[4,1,128]{2,1,0:T(1,128)S(1)} %get-tuple-element.536), channel_id=1, source_target_pairs={{0,1},{1,2},{2,3},{4,5},{5,6},{6,7},{8,9},{9,10},{10,11},{12,13},{... | collective-permute-start | bytes 6152 | tf_op jit(solution)/shard_map/while/body/eval_jaxpr/ppermute | solution.py:21
  (92 other events, 2302.2 us)
where the time goes:
time: 876 us; the launch traced here: 873 us
  starting transfers between devices  387 us (44%)
  matrix products  354 us (40%)
  local copies, waits for them, and re-layouts  65.3 us (7%)
  other arithmetic  52.7 us (6%)
    dot_general x42, matrix products, place_values(): lax.dot_general(row_onehot, weighted, (((0,), (0,)), ((), ())), precision...  137 us
    dot_general x42, matrix products, pick_values(): jnp.dot(row_onehot, table, precision=lax.Precision.HIGHEST, preferred_ele...  132 us
    ppermute x28, starting transfers between devices, extended(): lax.ppermute(first, axis, [(b, a) for a, b in up])  113 us
    all_to_all x14, starting transfers between devices, trade_both(): lax.all_to_all(paired, ('slab', 'plane'), split_axis=1, concat_axis=1, ti...  106 us
    ppermute x28, starting transfers between devices, extended(): lax.ppermute(last, axis, up)  75.9 us
    ppermute x14, starting transfers between devices, with_halo(): lax.ppermute(lax.slice_in_dim(block, block.shape[dim] - width, None, axis...  47.3 us
    dot_general x28, matrix products, membrane(): jnp.tensordot(gate_cond * gate_rev, renewed, axes=1, precision=lax.Precis...  42.3 us
    dot_general x28, matrix products, membrane(): jnp.tensordot(gate_cond, renewed, axes=1, precision=lax.Precision.HIGHEST)  42.3 us
  transfers between devices with their start and end apart: 99, of which 1 were waited for; matrix products, arithmetic and copies ran while one was open for 34% of the time, Pallas kernels for 0%

commit v1 on v0

v1 whole, which is shorter than its diff:
```python
import jax
import jax.numpy as jnp
from jax import lax
from jax.experimental import pallas as pl
from jax.experimental.pallas import tpu as pltpu
from jax.sharding import PartitionSpec as P

STEPS = 14
DT = 0.1
LN = 128
NV = 8
ROWS = 64
BLOCK = 2
VLIMIT = 8 * 1024 * 1024


def lane_iota():
    return lax.broadcasted_iota(jnp.int32, (8, LN), 1)


def sub_iota():
    return lax.broadcasted_iota(jnp.int32, (8, LN), 0)


def take(source, lanes):
    return jnp.take_along_axis(source, lanes, axis=1, mode="promise_in_bounds")


def gather_pair(tables, rows_refs, lane_refs, emit):
    def block(i, carry):
        for u in range(BLOCK):
            v = i * BLOCK + u
            at = pl.ds(pl.multiple_of(v * 8, 8), 8)
            for k, load in enumerate(tables):
                rows = rows_refs[k][at, :]
                lanes = lane_refs[k][at, :]
                total = jnp.zeros((8, LN), jnp.float32)
                for r in range(ROWS):
                    got = take(jnp.broadcast_to(load(r), (8, LN)), lanes)
                    total = jnp.where(rows == r, got, total)
                emit(k, v, at, total)
        return carry

    lax.fori_loop(0, NV // BLOCK, block, 0)


def plain_row(ref):
    return lambda r: ref[r : r + 1, :]


def fibre_row(ref):
    def load(r):
        f = (r // 32) * 8 + r % 8
        q = (r // 8) % 4
        return ref[f : f + 1, q * LN : (q + 1) * LN]

    return load


def step_eight(x, sub):
    turned = pltpu.roll(x, 1, axis=0)
    return jnp.where(sub == 0, pltpu.roll(turned, 1, axis=1), turned)


def earlier(values, k, sub):
    if k < 3:
        q = 1 << k
        return [values[v - q] if v >= q else step_eight(values[v - q + 8], sub) for v in range(NV)]
    if k < 6:
        q = 1 << (k - 3)
        out = []
        for x in values:
            turned = pltpu.roll(x, q, axis=0)
            out.append(jnp.where(sub < q, pltpu.roll(turned, 1, axis=1), turned))
        return out
    return [pltpu.roll(x, 1 << (k - 6), axis=1) for x in values]


def scan_steps(values, offs, ks, sub):
    for k in ks:
        before = earlier(values, k, sub)
        values = [x + jnp.where(o >= (1 << k), b, 0.0) for x, o, b in zip(values, offs, before)]
    return values


def load_list(ref):
    return [ref[8 * v : 8 * v + 8, :] for v in range(NV)]


def store_list(ref, values):
    for v, x in enumerate(values):
        ref[8 * v : 8 * v + 8, :] = x


def segment_sums(slot_refs, srow, slane, off, erow, elane, work, emit):
    tables = [plain_row(ref) for ref in slot_refs]

    def keep(k, v, at, total):
        work[k][at, :] = total

    gather_pair(tables, srow, slane, keep)
    sub = sub_iota()
    for k, ref in enumerate(work):
        offs = load_list(off[k])
        store_list(ref, scan_steps(load_list(ref), offs, range(3), sub))
        longest = offs[0]
        for o in offs[1:]:
            longest = jnp.maximum(longest, o)

        @pl.when(jnp.max(longest) >= 8)
        def _(ref=ref, offs=offs):
            store_list(ref, scan_steps(load_list(ref), offs, range(3, 13), sub))

    gather_pair([plain_row(ref) for ref in work], erow, elane, emit)


def sort_positions(values, lane, sub):
    def bit_mask(m):
        if m < 3:
            return None
        return ((sub >> (m - 3)) & 1) == 1 if m < 6 else ((lane >> (m - 6)) & 1) == 1

    for m in range(1, 14):
        for b in range(m - 1, -1, -1):
            down = bit_mask(m) if 3 <= m < 13 else None
            if b < 3:
                out = list(values)
                for v in range(NV):
                    w = v | (1 << b)
                    if v == w:
                        continue
                    lo = jnp.minimum(values[v], values[w])
                    hi = jnp.maximum(values[v], values[w])
                    if down is not None:
                        out[v] = jnp.where(down, hi, lo)
                        out[w] = jnp.where(down, lo, hi)
                    elif m < 3 and (v >> m) & 1:
                        out[v], out[w] = hi, lo
                    else:
                        out[v], out[w] = lo, hi
                values = out
            else:
                axis = 0 if b < 6 else 1
                d = 1 << (b - 3) if b < 6 else 1 << (b - 6)
                size = 8 if b < 6 else LN
                upper = bit_mask(b)
                keep_high = upper if down is None else jnp.logical_xor(upper, down)
                out = []
                for x in values:
                    partner = jnp.where(upper, pltpu.roll(x, d, axis=axis), pltpu.roll(x, size - d, axis=axis))
                    out.append(jnp.where(keep_high, jnp.maximum(x, partner), jnp.minimum(x, partner)))
                values = out
    return values


def prep_kernel(cell, gain, count, srow, slane, off, erow, elane, total, work):
    lane, sub = lane_iota(), sub_iota()
    cells = load_list(cell)
    keys = []
    for v in range(NV):
        slot = (v * 8 + sub) * LN + lane
        keys.append(jnp.where(cells[v] < 0, ROWS * LN, cells[v]) * (ROWS * LN) + slot)
    keys = sort_positions(keys, lane, sub)
    slots = [x & (ROWS * LN - 1) for x in keys]
    store_list(srow, [x >> 7 for x in slots])
    store_list(slane, [x & (LN - 1) for x in slots])
    owner = [x >> 13 for x in keys]
    place = [v + 8 * sub + 64 * lane for v in range(NV)]
    before = earlier(owner, 0, sub)
    first = [jnp.where((o != b) | (p == 0), p, 0) for o, b, p in zip(owner, before, place)]
    for k in range(13):
        prior = earlier(first, k, sub)
        first = [jnp.maximum(x, jnp.where(p >= (1 << k), y, 0)) for x, y, p in zip(first, prior, place)]
    filled = [o < ROWS * LN for o in owner]
    store_list(off, [jnp.where(ok, p - f, 0) for ok, p, f in zip(filled, place, first)])

    counts = load_list(count)
    run = []
    for x in counts:
        for k in range(7):
            x = x + jnp.where(lane >= (1 << k), pltpu.roll(x, 1 << k, axis=1), 0)
        run.append(x)
    base = jnp.zeros((8, LN), jnp.int32)
    ends_row, ends_lane = [], []
    for v in range(NV):
        rowsum = jnp.broadcast_to(run[v][:, LN - 1 :], (8, LN))
        upto = rowsum
        for k in range(3):
            upto = upto + jnp.where(sub >= (1 << k), pltpu.roll(upto, 1 << k, axis=0), 0)
        last = run[v] + upto - rowsum + base - 1
        ends_row.append(jnp.where(counts[v] > 0, 8 * (last & 7) + ((last >> 3) & 7), -1))
        ends_lane.append(jnp.where(counts[v] > 0, last >> 6, 0))
        base = base + jnp.broadcast_to(upto[7:8, :], (8, LN))
    store_list(erow, ends_row)
    store_list(elane, ends_lane)

    def emit(k, v, at, value):
        total[at, :] = value

    segment_sums([gain], [srow], [slane], [off], [erow], [elane], [work], emit)


def vspec():
    return pl.BlockSpec(memory_space=pltpu.VMEM)


def sspec():
    return pl.BlockSpec(memory_space=pltpu.SMEM)


def f32(*shape):
    return jax.ShapeDtypeStruct(shape, jnp.float32)


def i32(*shape):
    return jax.ShapeDtypeStruct(shape, jnp.int32)


def call(kernel, name, outs, specs, scratch=(), aliases=None):
    return pl.pallas_call(
        kernel,
        name=name,
        out_shape=outs,
        in_specs=specs,
        out_specs=tuple(vspec() for _ in outs),
        scratch_shapes=list(scratch),
        input_output_aliases=aliases or {},
        compiler_params=pltpu.CompilerParams(vmem_limit_bytes=VLIMIT),
    )


def prepare(cell, gain, count):
    table = i32(ROWS, LN)
    return call(
        prep_kernel,
        "prep",
        (table, table, table, table, table, f32(ROWS, LN)),
        [vspec()] * 3,
        [pltpu.VMEM((ROWS, LN), jnp.float32)],
    )(cell, gain, count)


def emit_messages(vt, vf, frow, flane, crow, clane, gslot, send, zup, zdn, yup, ydn):
    lane = lane_iota()
    parts = {}

    def emit(k, v, at, value):
        high = pl.ds(pl.multiple_of(v * 8 + ROWS, 8), 8)
        if k == 0:
            parts["fibre"] = value * gslot[at, :]
            return
        fib = parts["fibre"]
        send[at, :] = jnp.where(lane < 64, fib, pltpu.roll(value, 64, axis=1))
        send[high, :] = jnp.where(lane < 64, pltpu.roll(fib, 64, axis=1), value)

    gather_pair([fibre_row(vf), plain_row(vt)], [frow, crow], [flane, clane], emit)
    zup[...] = vt[48:64, :]
    zdn[...] = vt[0:16, :]
    yup[0:16, :] = vf[:, 384:512]
    ydn[0:16, :] = vf[:, 0:128]
    for z in range(4):
        yup[16 + z : 17 + z, :] = vt[16 * z + 15 : 16 * z + 16, :]
        ydn[16 + z : 17 + z, :] = vt[16 * z : 16 * z + 1, :]
    yup[20:24, :] = jnp.zeros((4, LN), jnp.float32)
    ydn[20:24, :] = jnp.zeros((4, LN), jnp.float32)


def first_kernel(vt, vf, frow, flane, crow, clane, gslot, send, zup, zdn, yup, ydn):
    emit_messages(vt, vf, frow, flane, crow, clane, gslot, send, zup, zdn, yup, ydn)


def exchange_kernel(
    recv, pt, pf, gslot,
    t_srow, t_slane, t_off, t_erow, t_elane,
    f_srow, f_slane, f_off, f_erow, f_elane,
    frow, flane, crow, clane,
    vt, vf, send, zup, zdn, yup, ydn,
    slot_t, slot_f, work_t, work_f,
):
    lane = lane_iota()
    for v in range(NV):
        low = recv[8 * v : 8 * v + 8, :]
        high = recv[ROWS + 8 * v : ROWS + 8 * v + 8, :]
        slot_t[8 * v : 8 * v + 8, :] = jnp.where(lane < 64, low, pltpu.roll(high, 64, axis=1))
        slot_f[8 * v : 8 * v + 8, :] = jnp.where(lane < 64, pltpu.roll(low, 64, axis=1), high) * gslot[8 * v : 8 * v + 8, :]

    def emit(k, v, at, value):
        if k == 0:
            vt[at, :] = pt[at, :] + DT * value
        else:
            fib = pl.ds(pl.multiple_of((v // 4) * 8, 8), 8)
            col = pl.ds(pl.multiple_of((v % 4) * LN, LN), LN)
            vf[fib, col] = pf[fib, col] + DT * value

    segment_sums(
        [slot_t, slot_f], [t_srow, f_srow], [t_slane, f_slane], [t_off, f_off],
        [t_erow, f_erow], [t_elane, f_elane], [work_t, work_f], emit,
    )
    emit_messages(vt, vf, frow, flane, crow, clane, gslot, send, zup, zdn, yup, ydn)


MESSAGES = (f32(128, LN), f32(16, LN), f32(16, LN), f32(24, LN), f32(24, LN))


def membrane_kernel(par, vt, vf, gt_in, gf_in, gt, gf, ion_t, ion_f):
    def one(v, old, k):
        gate = old
        t1 = jnp.tanh(0.5 * v - par[0, k])
        th = jnp.tanh(v - par[1, k])
        steady = 0.5 + (0.5 if k % 2 == 0 else -0.5) * th
        factor = jnp.exp2(par[2, k] + par[3, k] * t1)
        return steady + (gate - steady) * factor

    def block(b, carry):
        at = pl.ds(pl.multiple_of(b * 8, 8), 8)
        fib = pl.ds(pl.multiple_of((b // 4) * 8, 8), 8)
        col = pl.ds(pl.multiple_of((b % 4) * LN, LN), LN)
        v = vt[at, :]
        w = vf[fib, col]
        st = jnp.zeros((8, LN), jnp.float32)
        dt_ = st
        sf = st
        df = st
        for k in range(gt.shape[0]):
            a = one(v, gt_in[k, at, :], k)
            gt[k, at, :] = a
            st = st + par[4, k] * a
            dt_ = dt_ + par[5, k] * a
            c = one(w, gf_in[k, fib, col], k)
            gf[k, fib, col] = c
            sf = sf + par[4, k] * c
            df = df + par[5, k] * c
        ion_t[at, :] = v * st - dt_
        ion_f[fib, col] = w * sf - df
        return carry

    lax.fori_loop(0, NV, block, 0)


def combine_kernel(edge, vt, vf, ion_t, ion_f, diff_t, diff_f, sum_t, sum_f, zlo, zhi, ylo, yhi, pt, pf):
    lane = lax.broadcasted_iota(jnp.int32, (16, LN), 1)
    row = lax.broadcasted_iota(jnp.int32, (16, LN), 0)
    not_first = jnp.where(lane > 0, 1.0, 0.0)
    not_last = jnp.where(lane < LN - 1, 1.0, 0.0)
    for z in range(4):
        here = vt[16 * z : 16 * z + 16, :]
        below = vt[16 * z - 16 : 16 * z, :] if z > 0 else zlo[...] * edge[0]
        above = vt[16 * z + 16 : 16 * z + 32, :] if z < 3 else zhi[...] * edge[1]
        front = jnp.broadcast_to(ylo[16 + z : 17 + z, :] * edge[2], (16, LN))
        back = jnp.broadcast_to(yhi[16 + z : 17 + z, :] * edge[3], (16, LN))
        left_y = jnp.where(row == 0, front, pltpu.roll(here, 1, axis=0))
        right_y = jnp.where(row == 15, back, pltpu.roll(here, 15, axis=0))
        left_x = pltpu.roll(here, 1, axis=1) * not_first
        right_x = pltpu.roll(here, LN - 1, axis=1) * not_last
        count = not_first + not_last + jnp.where(row == 0, edge[2], 1.0) + jnp.where(row == 15, edge[3], 1.0)
        count = count + (edge[0] if z == 0 else 1.0) + (edge[1] if z == 3 else 1.0)
        lap = below + above + left_y + right_y + left_x + right_x - count * here
        at = slice(16 * z, 16 * z + 16)
        pt[at, :] = here + DT * (diff_t[at, :] * lap - ion_t[at, :] - sum_t[at, :] * here)
    for q in range(4):
        at = slice(q * LN, (q + 1) * LN)
        here = vf[:, at]
        prior = vf[:, (q - 1) * LN : q * LN] if q > 0 else ylo[0:16, :] * edge[2]
        after = vf[:, (q + 1) * LN : (q + 2) * LN] if q < 3 else yhi[0:16, :] * edge[3]
        left = jnp.where(lane == 0, pltpu.roll(prior, 1, axis=1), pltpu.roll(here, 1, axis=1))
        right = jnp.where(lane == LN - 1, pltpu.roll(after, LN - 1, axis=1), pltpu.roll(here, LN - 1, axis=1))
        count = jnp.full((16, LN), 2.0, jnp.float32)
        if q == 0:
            count = count - jnp.where(lane == 0, 1.0 - edge[2], 0.0)
        if q == 3:
            count = count - jnp.where(lane == LN - 1, 1.0 - edge[3], 0.0)
        lap = left + right - count * here
        fsum = jnp.concatenate([sum_f[8 * q : 8 * q + 8, :], sum_f[32 + 8 * q : 40 + 8 * q, :]], axis=0)
        pf[:, at] = here + DT * (diff_f[:, at] * lap - ion_f[:, at] - fsum * here)


def make_onehot(indices, count):
    return (indices[:, None] == jnp.arange(count, dtype=jnp.int32)[None, :]).astype(jnp.float32)


def place_values(row_onehot, col_onehot, values):
    return lax.dot_general(
        row_onehot, col_onehot * values[:, None], (((0,), (0,)), ((), ())),
        precision=lax.Precision.HIGHEST, preferred_element_type=jnp.float32,
    )


def cell_counts(cells):
    rows = jnp.where(cells < 0, -1, cells // LN).reshape(-1)
    cols = jnp.where(cells < 0, -1, cells % LN).reshape(-1)
    counts = lax.dot_general(
        make_onehot(rows, ROWS), make_onehot(cols, LN), (((0,), (0,)), ((), ())),
        preferred_element_type=jnp.float32,
    )
    return counts.astype(jnp.int32)


def fold(pairs):
    return jnp.concatenate([pairs[:64], pairs[64:]], axis=1)


def split_cells(cells):
    return jnp.where(cells < 0, -1, cells >> 7), jnp.where(cells < 0, 0, cells & (LN - 1))


def body(
    tissue_v, tissue_gates, tissue_diff, fibre_v, fibre_gates, fibre_diff,
    gate_half, gate_rate, gate_cond, gate_rev, junc_cond,
    junc_fibre, junc_fcell, junc_owner, junc_tcell, junc_class,
):
    slabs = lax.axis_size("slab")
    planes = lax.axis_size("plane")
    devices = slabs * planes
    gates = tissue_gates.shape[0]
    capacity = 64
    vt = tissue_v.reshape(ROWS, LN)
    diff_t = tissue_diff.reshape(ROWS, LN)
    gt = tissue_gates.reshape(gates, ROWS, LN)

    owners = junc_owner[:, 0]
    owner_onehot = make_onehot(owners, devices)
    owner_table = owner_onehot.astype(jnp.int32)
    rank = jnp.sum(jnp.cumsum(owner_table, axis=0) * owner_table, axis=1) - 1
    rank_onehot = make_onehot(rank, capacity)
    gain = jnp.sum(
        jnp.where(
            junc_class[:, None] == jnp.arange(junc_cond.shape[0], dtype=jnp.int32)[None, :],
            junc_cond[None, :], jnp.zeros((), jnp.float32),
        ),
        axis=1,
    )
    fibre_id = ((junc_fibre // 8) * 32 + (junc_fcell // LN) * 8 + junc_fibre % 8) * LN + junc_fcell % LN
    slot_fibre = place_values(owner_onehot, rank_onehot, (fibre_id + 1).astype(jnp.float32))
    slot_cell = place_values(owner_onehot, rank_onehot, (junc_tcell + 1).astype(jnp.float32))
    slot_gain = place_values(owner_onehot, rank_onehot, gain)
    sent = jnp.concatenate([slot_cell, slot_gain], axis=1)
    got = lax.all_to_all(sent, ("slab", "plane"), split_axis=0, concat_axis=0, tiled=True)

    fcells = fold(slot_fibre).astype(jnp.int32) - 1
    gslot = fold(slot_gain)
    frow, flane = split_cells(fcells)
    f_srow, f_slane, f_off, f_erow, f_elane, sum_f = prepare(fcells, gslot, cell_counts(fcells))
    tcells = fold(got[:, :64]).astype(jnp.int32) - 1
    tgain = fold(got[:, 64:])
    crow, clane = split_cells(tcells)
    t_srow, t_slane, t_off, t_erow, t_elane, sum_t = prepare(tcells, tgain, cell_counts(tcells))

    log2e = 1.4426950408889634
    par = jnp.stack(
        [
            0.5 * gate_half, gate_half,
            (-1.5 * DT * log2e) * gate_rate, (-0.5 * DT * log2e) * gate_rate,
            gate_cond, gate_cond * gate_rev,
        ]
    )
    s, p = lax.axis_index("slab"), lax.axis_index("plane")
    edge = jnp.stack([s > 0, s < slabs - 1, p > 0, p < planes - 1]).astype(jnp.float32)

    def ring(axis, shift):
        n = lax.axis_size(axis)
        return [(i, (i + shift) % n) for i in range(n)]

    messages = call(first_kernel, "first", MESSAGES, [vspec()] * 7)(vt, fibre_v, frow, flane, crow, clane, gslot)

    def advance(i, carry):
        vt, vf, gt, gf, send, zup, zdn, yup, ydn = carry
        recv = lax.all_to_all(send, ("slab", "plane"), split_axis=0, concat_axis=0, tiled=True)
        zlo = lax.ppermute(zup, "slab", ring("slab", 1))
        zhi = lax.ppermute(zdn, "slab", ring("slab", -1))
        ylo = lax.ppermute(yup, "plane", ring("plane", 1))
        yhi = lax.ppermute(ydn, "plane", ring("plane", -1))
        gt, gf, ion_t, ion_f = call(
            membrane_kernel, "membrane",
            (f32(gates, ROWS, LN), f32(gates, 16, 512), f32(ROWS, LN), f32(16, 512)),
            [sspec()] + [vspec()] * 4, aliases={3: 0, 4: 1},
        )(par, vt, vf, gt, gf)
        pt, pf = call(
            combine_kernel, "combine", (f32(ROWS, LN), f32(16, 512)), [sspec()] + [vspec()] * 12
        )(edge, vt, vf, ion_t, ion_f, diff_t, fibre_diff, sum_t, sum_f, zlo, zhi, ylo, yhi)
        out = call(
            exchange_kernel, "exchange", (f32(ROWS, LN), f32(16, 512)) + MESSAGES, [vspec()] * 18,
            [pltpu.VMEM((ROWS, LN), jnp.float32)] * 4,
        )(
            recv, pt, pf, gslot,
            t_srow, t_slane, t_off, t_erow, t_elane,
            f_srow, f_slane, f_off, f_erow, f_elane,
            frow, flane, crow, clane,
        )
        return (out[0], out[1], gt, gf) + tuple(out[2:])

    final = lax.fori_loop(0, STEPS, advance, (vt, fibre_v, gt, fibre_gates) + tuple(messages))
    return final[0].reshape(tissue_v.shape), final[1]


def solution(mesh):
    in_specs = (
        P("slab", "plane", None),
        P(None, "slab", "plane", None),
        P("slab", "plane", None),
        P("slab", "plane"),
        P(None, "slab", "plane"),
        P("slab", "plane"),
        P(),
        P(),
        P(),
        P(),
        P(),
        P(("slab", "plane")),
        P(("slab", "plane")),
        P(("slab", "plane"), None),
        P(("slab", "plane")),
        P(("slab", "plane")),
    )
    out_specs = (P("slab", "plane", None), P("slab", "plane"))
    return jax.shard_map(body, mesh=mesh, in_specs=in_specs, out_specs=out_specs, check_vma=False)
```

time: 876 us -> 396 us (0.45)
  matrix products: 354 us -> 13.3 us
  starting transfers between devices: 387 us -> 212 us
  Pallas kernels: 0 us -> 148 us
  local copies, waits for them, and re-layouts: 65.3 us -> 5.33 us
  other arithmetic: 52.7 us -> 3.18 us
    dot_general x140 -> x5, matrix products: 354 us -> 13.3 us  [the longest x3 10.7 us: place_values(): lax.dot_general(row_onehot, col_onehot * values[:, None], (((0,), (0,)),...]
    ppermute x84 -> x56, starting transfers between devices: 271 us -> 83.3 us  [the longest x14 53.9 us: advance(): zhi = lax.ppermute(zdn, 'slab', ring('slab', -1))]
    pallas_call x0 -> x45, Pallas kernels: none -> 148 us  [the longest x14 82.5 us: advance(): call(exchange_kernel, 'exchange', (f32(ROWS, LN), f32(16, 512)) + MESSAGE...]
    add x74 -> x0, other arithmetic: 37.6 us -> none  [the longest x28 34.6 us: membrane(): renewed = steady + (gates - steady) * decay_factor]
    scatter x2 -> x0, local copies, waits for them, and re-layouts: 31.4 us -> none  [the longest x1 15.9 us: body(): jnp.zeros((devices * capacity,), jnp.int32).at[slot_index].set(junc_tcell)]
    all_to_all x15, starting transfers between devices: 116 us -> 129 us  [the longest x14 118 us: advance(): lax.all_to_all(send, ('slab', 'plane'), split_axis=0, concat_axis=0, tile...]
    while x84 -> x0, local copies, waits for them, and re-layouts: 12.8 us -> none
    all_to_all x15 -> x1, other arithmetic: 12 us -> 0.01 us  [body(): lax.all_to_all(sent, ('slab', 'plane'), split_axis=0, concat_axis=0, tile...]
  transfers between devices with their start and end apart: 99 -> 71, of which waited for: 1 -> 1; matrix products, arithmetic and copies ran while one was open for 34% -> 0% of each run, Pallas kernels for 0% -> 14%
where the time goes in v1:
time: 396 us; the launch traced here: 392 us
  starting transfers between devices  212 us (54%)
  Pallas kernels  148 us (37%)
  matrix products  13.3 us (3%)
  waiting for transfers between devices  7.97 us (2%)
  local copies, waits for them, and re-layouts  5.33 us (1%)
    all_to_all x14, starting transfers between devices, advance(): lax.all_to_all(send, ('slab', 'plane'), split_axis=0, concat_axis=0, tile...  118 us
    pallas_call x14, Pallas kernels, advance(): call(exchange_kernel, 'exchange', (f32(ROWS, LN), f32(16, 512)) + MESSAGE...  82.5 us
    ppermute x14, starting transfers between devices, advance(): zhi = lax.ppermute(zdn, 'slab', ring('slab', -1))  53.9 us
    pallas_call x14, Pallas kernels, advance(): call(membrane_kernel, 'membrane', (f32(gates, ROWS, LN), f32(gates, 16, 5...  43.9 us
    ppermute x14, starting transfers between devices, advance(): ylo = lax.ppermute(yup, 'plane', ring('plane', 1))  21.7 us
    dot_general x3, matrix products, place_values(): lax.dot_general(row_onehot, col_onehot * values[:, None], (((0,), (0,)),...  10.7 us
    all_to_all x1, starting transfers between devices, body(): lax.all_to_all(sent, ('slab', 'plane'), split_axis=0, concat_axis=0, tile...  10.2 us
    pallas_call x2, Pallas kernels, prepare(): call(prep_kernel, 'prep', (table, table, table, table, table, f32(ROWS, L...  10.1 us
  transfers between devices with their start and end apart: 71, of which 1 were waited for; matrix products, arithmetic and copies ran while one was open for 0% of the time, Pallas kernels for 14%

profile of v1, /device:TPU:34, one launch (start us, length us, event | category | flops | bytes accessed | tf_op | source)
XLA Modules:
  0.0 391.9 jit_solution(3603665739858408428)
XLA Ops:
  25.6 10.2 %all-to-all-start.1 = ((f32[128,1,128]{2,1,0:T(1,128)}), f32[128,1,128]{2,1,0:T(1,128)S(1)}, u32[]{:S(2)}, u32[]{:S(2)}) async-start(f32[128,1,128]{2,1,0:T(1,128)} %copy.53), calls=%async_computation.1 | async-start | bytes 131072 | tf_op jit(solution)/shard_map/all_to_all | solution.py:437
  35.9 7.8 %all-to-all-done.1 = f32[128,1,128]{2,1,0:T(1,128)S(1)} async-done(((f32[128,1,128]{2,1,0:T(1,128)}), f32[128,1,128]{2,1,0:T(1,128)S(1)}, u32[]{:S(2)}, u32[]{:S(2)}) %all-to-all-start.1) | async-done | bytes 65568 | tf_op jit(solution)/shard_map/all_to_all | solution.py:437
  52.8 338.4 %while.26 = (s32[]{:T(128)}, f32[64,128]{1,0:T(8,128)S(1)}, f32[16,512]{1,0:T(8,128)S(1)}, f32[40,64,128]{2,1,0:T(8,128)S(1)}, f32[40,16,512]{2,1,0:T(8,128)S(1)...) while((s32[]{:T(128)}, f32[64,128]{1,0:T(8,128)S(1)}, ...), condition=%wide.region_5.6_spmd, body=%wide.region_4.5_spmd.sunk | while | flops 2 | bytes 360917 | solution.py:491
  52.8 6.1 %all-to-all-start = ((f32[128,1,128]{2,1,0:T(1,128)}), f32[128,1,128]{2,1,0:T(1,128)S(1)}, u32[]{:S(2)}, u32[]{:S(2)}) async-start(f32[128,1,128]{2,1,0:T(1,128)} %bitcast.75), calls=%async_computation | async-start | bytes 131072 | tf_op jit(solution)/shard_map/while/body/eval_jaxpr/all_to_all | solution.py:467
  68.8 5.9 %exchange.1 = (f32[64,128]{1,0:T(8,128)S(1)}, f32[16,512]{1,0:T(8,128)S(1)}, f32[128,128]{1,0:T(8,128)}, f32[16,128]{1,0:T(8,128)S(1)}, f32[16,128]{1,0:T(8,128)...) custom-call(f32[128,128]{1,0:T(8,128)S(1)} %bitcast.77, f32[64,128]{1,0:T(8,128)S(1)} %get-tuple-element.494.pt, ...), custom_call_target="tpu_custom_call" | custom-call | tf_op jit(solution)/shard_map/while/body/eval_jaxpr/exchange/pallas_call | solution.py:480
  74.7 8.6 %all-to-all-start = ((f32[128,1,128]{2,1,0:T(1,128)}), f32[128,1,128]{2,1,0:T(1,128)S(1)}, u32[]{:S(2)}, u32[]{:S(2)}) async-start(f32[128,1,128]{2,1,0:T(1,128)} %bitcast.75), calls=%async_computation | async-start | bytes 131072 | tf_op jit(solution)/shard_map/while/body/eval_jaxpr/all_to_all | solution.py:467
  99.0 8.6 %all-to-all-start = ((f32[128,1,128]{2,1,0:T(1,128)}), f32[128,1,128]{2,1,0:T(1,128)S(1)}, u32[]{:S(2)}, u32[]{:S(2)}) async-start(f32[128,1,128]{2,1,0:T(1,128)} %bitcast.75), calls=%async_computation | async-start | bytes 131072 | tf_op jit(solution)/shard_map/while/body/eval_jaxpr/all_to_all | solution.py:467
  117.5 5.9 %exchange.1 = (f32[64,128]{1,0:T(8,128)S(1)}, f32[16,512]{1,0:T(8,128)S(1)}, f32[128,128]{1,0:T(8,128)}, f32[16,128]{1,0:T(8,128)S(1)}, f32[16,128]{1,0:T(8,128)...) custom-call(f32[128,128]{1,0:T(8,128)S(1)} %bitcast.77, f32[64,128]{1,0:T(8,128)S(1)} %get-tuple-element.494.pt, ...), custom_call_target="tpu_custom_call" | custom-call | tf_op jit(solution)/shard_map/while/body/eval_jaxpr/exchange/pallas_call | solution.py:480
  123.4 8.6 %all-to-all-start = ((f32[128,1,128]{2,1,0:T(1,128)}), f32[128,1,128]{2,1,0:T(1,128)S(1)}, u32[]{:S(2)}, u32[]{:S(2)}) async-start(f32[128,1,128]{2,1,0:T(1,128)} %bitcast.75), calls=%async_computation | async-start | bytes 131072 | tf_op jit(solution)/shard_map/while/body/eval_jaxpr/all_to_all | solution.py:467
  141.8 5.9 %exchange.1 = (f32[64,128]{1,0:T(8,128)S(1)}, f32[16,512]{1,0:T(8,128)S(1)}, f32[128,128]{1,0:T(8,128)}, f32[16,128]{1,0:T(8,128)S(1)}, f32[16,128]{1,0:T(8,128)...) custom-call(f32[128,128]{1,0:T(8,128)S(1)} %bitcast.77, f32[64,128]{1,0:T(8,128)S(1)} %get-tuple-element.494.pt, ...), custom_call_target="tpu_custom_call" | custom-call | tf_op jit(solution)/shard_map/while/body/eval_jaxpr/exchange/pallas_call | solution.py:480
  147.7 8.6 %all-to-all-start = ((f32[128,1,128]{2,1,0:T(1,128)}), f32[128,1,128]{2,1,0:T(1,128)S(1)}, u32[]{:S(2)}, u32[]{:S(2)}) async-start(f32[128,1,128]{2,1,0:T(1,128)} %bitcast.75), calls=%async_computation | async-start | bytes 131072 | tf_op jit(solution)/shard_map/while/body/eval_jaxpr/all_to_all | solution.py:467
  166.2 5.9 %exchange.1 = (f32[64,128]{1,0:T(8,128)S(1)}, f32[16,512]{1,0:T(8,128)S(1)}, f32[128,128]{1,0:T(8,128)}, f32[16,128]{1,0:T(8,128)S(1)}, f32[16,128]{1,0:T(8,128)...) custom-call(f32[128,128]{1,0:T(8,128)S(1)} %bitcast.77, f32[64,128]{1,0:T(8,128)S(1)} %get-tuple-element.494.pt, ...), custom_call_target="tpu_custom_call" | custom-call | tf_op jit(solution)/shard_map/while/body/eval_jaxpr/exchange/pallas_call | solution.py:480
  172.1 8.6 %all-to-all-start = ((f32[128,1,128]{2,1,0:T(1,128)}), f32[128,1,128]{2,1,0:T(1,128)S(1)}, u32[]{:S(2)}, u32[]{:S(2)}) async-start(f32[128,1,128]{2,1,0:T(1,128)} %bitcast.75), calls=%async_computation | async-start | bytes 131072 | tf_op jit(solution)/shard_map/while/body/eval_jaxpr/all_to_all | solution.py:467
  196.4 8.6 %all-to-all-start = ((f32[128,1,128]{2,1,0:T(1,128)}), f32[128,1,128]{2,1,0:T(1,128)S(1)}, u32[]{:S(2)}, u32[]{:S(2)}) async-start(f32[128,1,128]{2,1,0:T(1,128)} %bitcast.75), calls=%async_computation | async-start | bytes 131072 | tf_op jit(solution)/shard_map/while/body/eval_jaxpr/all_to_all | solution.py:467
  214.9 5.9 %exchange.1 = (f32[64,128]{1,0:T(8,128)S(1)}, f32[16,512]{1,0:T(8,128)S(1)}, f32[128,128]{1,0:T(8,128)}, f32[16,128]{1,0:T(8,128)S(1)}, f32[16,128]{1,0:T(8,128)...) custom-call(f32[128,128]{1,0:T(8,128)S(1)} %bitcast.77, f32[64,128]{1,0:T(8,128)S(1)} %get-tuple-element.494.pt, ...), custom_call_target="tpu_custom_call" | custom-call | tf_op jit(solution)/shard_map/while/body/eval_jaxpr/exchange/pallas_call | solution.py:480
  220.8 8.6 %all-to-all-start = ((f32[128,1,128]{2,1,0:T(1,128)}), f32[128,1,128]{2,1,0:T(1,128)S(1)}, u32[]{:S(2)}, u32[]{:S(2)}) async-start(f32[128,1,128]{2,1,0:T(1,128)} %bitcast.75), calls=%async_computation | async-start | bytes 131072 | tf_op jit(solution)/shard_map/while/body/eval_jaxpr/all_to_all | solution.py:467
  239.2 5.9 %exchange.1 = (f32[64,128]{1,0:T(8,128)S(1)}, f32[16,512]{1,0:T(8,128)S(1)}, f32[128,128]{1,0:T(8,128)}, f32[16,128]{1,0:T(8,128)S(1)}, f32[16,128]{1,0:T(8,128)...) custom-call(f32[128,128]{1,0:T(8,128)S(1)} %bitcast.77, f32[64,128]{1,0:T(8,128)S(1)} %get-tuple-element.494.pt, ...), custom_call_target="tpu_custom_call" | custom-call | tf_op jit(solution)/shard_map/while/body/eval_jaxpr/exchange/pallas_call | solution.py:480
  245.1 8.6 %all-to-all-start = ((f32[128,1,128]{2,1,0:T(1,128)}), f32[128,1,128]{2,1,0:T(1,128)S(1)}, u32[]{:S(2)}, u32[]{:S(2)}) async-start(f32[128,1,128]{2,1,0:T(1,128)} %bitcast.75), calls=%async_computation | async-start | bytes 131072 | tf_op jit(solution)/shard_map/while/body/eval_jaxpr/all_to_all | solution.py:467
  263.6 5.9 %exchange.1 = (f32[64,128]{1,0:T(8,128)S(1)}, f32[16,512]{1,0:T(8,128)S(1)}, f32[128,128]{1,0:T(8,128)}, f32[16,128]{1,0:T(8,128)S(1)}, f32[16,128]{1,0:T(8,128)...) custom-call(f32[128,128]{1,0:T(8,128)S(1)} %bitcast.77, f32[64,128]{1,0:T(8,128)S(1)} %get-tuple-element.494.pt, ...), custom_call_target="tpu_custom_call" | custom-call | tf_op jit(solution)/shard_map/while/body/eval_jaxpr/exchange/pallas_call | solution.py:480
  269.5 8.6 %all-to-all-start = ((f32[128,1,128]{2,1,0:T(1,128)}), f32[128,1,128]{2,1,0:T(1,128)S(1)}, u32[]{:S(2)}, u32[]{:S(2)}) async-start(f32[128,1,128]{2,1,0:T(1,128)} %bitcast.75), calls=%async_computation | async-start | bytes 131072 | tf_op jit(solution)/shard_map/while/body/eval_jaxpr/all_to_all | solution.py:467
  293.8 8.6 %all-to-all-start = ((f32[128,1,128]{2,1,0:T(1,128)}), f32[128,1,128]{2,1,0:T(1,128)S(1)}, u32[]{:S(2)}, u32[]{:S(2)}) async-start(f32[128,1,128]{2,1,0:T(1,128)} %bitcast.75), calls=%async_computation | async-start | bytes 131072 | tf_op jit(solution)/shard_map/while/body/eval_jaxpr/all_to_all | solution.py:467
  318.2 8.6 %all-to-all-start = ((f32[128,1,128]{2,1,0:T(1,128)}), f32[128,1,128]{2,1,0:T(1,128)S(1)}, u32[]{:S(2)}, u32[]{:S(2)}) async-start(f32[128,1,128]{2,1,0:T(1,128)} %bitcast.75), calls=%async_computation | async-start | bytes 131072 | tf_op jit(solution)/shard_map/while/body/eval_jaxpr/all_to_all | solution.py:467
  342.5 8.6 %all-to-all-start = ((f32[128,1,128]{2,1,0:T(1,128)}), f32[128,1,128]{2,1,0:T(1,128)S(1)}, u32[]{:S(2)}, u32[]{:S(2)}) async-start(f32[128,1,128]{2,1,0:T(1,128)} %bitcast.75), calls=%async_computation | async-start | bytes 131072 | tf_op jit(solution)/shard_map/while/body/eval_jaxpr/all_to_all | solution.py:467
  366.9 8.6 %all-to-all-start = ((f32[128,1,128]{2,1,0:T(1,128)}), f32[128,1,128]{2,1,0:T(1,128)S(1)}, u32[]{:S(2)}, u32[]{:S(2)}) async-start(f32[128,1,128]{2,1,0:T(1,128)} %bitcast.75), calls=%async_computation | async-start | bytes 131072 | tf_op jit(solution)/shard_map/while/body/eval_jaxpr/all_to_all | solution.py:467
  (233 shorter events, 212.4 us)
Async XLA Ops:
  25.6 18.1 %all-to-all-start.1 = ((f32[128,1,128]{2,1,0:T(1,128)}), f32[128,1,128]{2,1,0:T(1,128)S(1)}, u32[]{:S(2)}, u32[]{:S(2)}) async-start(f32[128,1,128]{2,1,0:T(1,128)} %copy.53), calls=%async_computation.1 | async-start | bytes 131072 | tf_op jit(solution)/shard_map/all_to_all | solution.py:437
  52.8 15.9 %all-to-all-start = ((f32[128,1,128]{2,1,0:T(1,128)}), f32[128,1,128]{2,1,0:T(1,128)S(1)}, u32[]{:S(2)}, u32[]{:S(2)}) async-start(f32[128,1,128]{2,1,0:T(1,128)} %bitcast.75), calls=%async_computation | async-start | bytes 131072 | tf_op jit(solution)/shard_map/while/body/eval_jaxpr/all_to_all | solution.py:467
  59.0 9.1 %collective-permute-start.2 = (f32[24,128]{1,0:T(8,128)S(1)}, f32[24,128]{1,0:T(8,128)S(1)}, u32[]{:S(2)}, u32[]{:S(2)}) collective-permute-start(f32[24,128]{1,0:T(8,128)S(1)} %get-tuple-element.545), channel_id=1, source_target_pairs={{0,1},{1,2},{2,3},{3,0},{4,5},{5,6},{6,7},{7,4},{8,9},{9,10},{10,1... | collective-permute-start | bytes 36872 | tf_op jit(solution)/shard_map/while/body/eval_jaxpr/ppermute | solution.py:470
  74.7 18.5 %all-to-all-start = ((f32[128,1,128]{2,1,0:T(1,128)}), f32[128,1,128]{2,1,0:T(1,128)S(1)}, u32[]{:S(2)}, u32[]{:S(2)}) async-start(f32[128,1,128]{2,1,0:T(1,128)} %bitcast.75), calls=%async_computation | async-start | bytes 131072 | tf_op jit(solution)/shard_map/while/body/eval_jaxpr/all_to_all | solution.py:467
  83.3 9.1 %collective-permute-start.2 = (f32[24,128]{1,0:T(8,128)S(1)}, f32[24,128]{1,0:T(8,128)S(1)}, u32[]{:S(2)}, u32[]{:S(2)}) collective-permute-start(f32[24,128]{1,0:T(8,128)S(1)} %get-tuple-element.545), channel_id=1, source_target_pairs={{0,1},{1,2},{2,3},{3,0},{4,5},{5,6},{6,7},{7,4},{8,9},{9,10},{10,1... | collective-permute-start | bytes 36872 | tf_op jit(solution)/shard_map/while/body/eval_jaxpr/ppermute | solution.py:470
  99.0 18.5 %all-to-all-start = ((f32[128,1,128]{2,1,0:T(1,128)}), f32[128,1,128]{2,1,0:T(1,128)S(1)}, u32[]{:S(2)}, u32[]{:S(2)}) async-start(f32[128,1,128]{2,1,0:T(1,128)} %bitcast.75), calls=%async_computation | async-start | bytes 131072 | tf_op jit(solution)/shard_map/while/body/eval_jaxpr/all_to_all | solution.py:467
  107.7 9.1 %collective-permute-start.2 = (f32[24,128]{1,0:T(8,128)S(1)}, f32[24,128]{1,0:T(8,128)S(1)}, u32[]{:S(2)}, u32[]{:S(2)}) collective-permute-start(f32[24,128]{1,0:T(8,128)S(1)} %get-tuple-element.545), channel_id=1, source_target_pairs={{0,1},{1,2},{2,3},{3,0},{4,5},{5,6},{6,7},{7,4},{8,9},{9,10},{10,1... | collective-permute-start | bytes 36872 | tf_op jit(solution)/shard_map/while/body/eval_jaxpr/ppermute | solution.py:470
  123.4 18.5 %all-to-all-start = ((f32[128,1,128]{2,1,0:T(1,128)}), f32[128,1,128]{2,1,0:T(1,128)S(1)}, u32[]{:S(2)}, u32[]{:S(2)}) async-start(f32[128,1,128]{2,1,0:T(1,128)} %bitcast.75), calls=%async_computation | async-start | bytes 131072 | tf_op jit(solution)/shard_map/while/body/eval_jaxpr/all_to_all | solution.py:467
  132.0 9.1 %collective-permute-start.2 = (f32[24,128]{1,0:T(8,128)S(1)}, f32[24,128]{1,0:T(8,128)S(1)}, u32[]{:S(2)}, u32[]{:S(2)}) collective-permute-start(f32[24,128]{1,0:T(8,128)S(1)} %get-tuple-element.545), channel_id=1, source_target_pairs={{0,1},{1,2},{2,3},{3,0},{4,5},{5,6},{6,7},{7,4},{8,9},{9,10},{10,1... | collective-permute-start | bytes 36872 | tf_op jit(solution)/shard_map/while/body/eval_jaxpr/ppermute | solution.py:470
  147.7 18.5 %all-to-all-start = ((f32[128,1,128]{2,1,0:T(1,128)}), f32[128,1,128]{2,1,0:T(1,128)S(1)}, u32[]{:S(2)}, u32[]{:S(2)}) async-start(f32[128,1,128]{2,1,0:T(1,128)} %bitcast.75), calls=%async_computation | async-start | bytes 131072 | tf_op jit(solution)/shard_map/while/body/eval_jaxpr/all_to_all | solution.py:467
  156.4 9.1 %collective-permute-start.2 = (f32[24,128]{1,0:T(8,128)S(1)}, f32[24,128]{1,0:T(8,128)S(1)}, u32[]{:S(2)}, u32[]{:S(2)}) collective-permute-start(f32[24,128]{1,0:T(8,128)S(1)} %get-tuple-element.545), channel_id=1, source_target_pairs={{0,1},{1,2},{2,3},{3,0},{4,5},{5,6},{6,7},{7,4},{8,9},{9,10},{10,1... | collective-permute-start | bytes 36872 | tf_op jit(solution)/shard_map/while/body/eval_jaxpr/ppermute | solution.py:470
  172.1 18.5 %all-to-all-start = ((f32[128,1,128]{2,1,0:T(1,128)}), f32[128,1,128]{2,1,0:T(1,128)S(1)}, u32[]{:S(2)}, u32[]{:S(2)}) async-start(f32[128,1,128]{2,1,0:T(1,128)} %bitcast.75), calls=%async_computation | async-start | bytes 131072 | tf_op jit(solution)/shard_map/while/body/eval_jaxpr/all_to_all | solution.py:467
  180.7 9.1 %collective-permute-start.2 = (f32[24,128]{1,0:T(8,128)S(1)}, f32[24,128]{1,0:T(8,128)S(1)}, u32[]{:S(2)}, u32[]{:S(2)}) collective-permute-start(f32[24,128]{1,0:T(8,128)S(1)} %get-tuple-element.545), channel_id=1, source_target_pairs={{0,1},{1,2},{2,3},{3,0},{4,5},{5,6},{6,7},{7,4},{8,9},{9,10},{10,1... | collective-permute-start | bytes 36872 | tf_op jit(solution)/shard_map/while/body/eval_jaxpr/ppermute | solution.py:470
  196.4 18.5 %all-to-all-start = ((f32[128,1,128]{2,1,0:T(1,128)}), f32[128,1,128]{2,1,0:T(1,128)S(1)}, u32[]{:S(2)}, u32[]{:S(2)}) async-start(f32[128,1,128]{2,1,0:T(1,128)} %bitcast.75), calls=%async_computation | async-start | bytes 131072 | tf_op jit(solution)/shard_map/while/body/eval_jaxpr/all_to_all | solution.py:467
  205.1 9.1 %collective-permute-start.2 = (f32[24,128]{1,0:T(8,128)S(1)}, f32[24,128]{1,0:T(8,128)S(1)}, u32[]{:S(2)}, u32[]{:S(2)}) collective-permute-start(f32[24,128]{1,0:T(8,128)S(1)} %get-tuple-element.545), channel_id=1, source_target_pairs={{0,1},{1,2},{2,3},{3,0},{4,5},{5,6},{6,7},{7,4},{8,9},{9,10},{10,1... | collective-permute-start | bytes 36872 | tf_op jit(solution)/shard_map/while/body/eval_jaxpr/ppermute | solution.py:470
  220.8 18.5 %all-to-all-start = ((f32[128,1,128]{2,1,0:T(1,128)}), f32[128,1,128]{2,1,0:T(1,128)S(1)}, u32[]{:S(2)}, u32[]{:S(2)}) async-start(f32[128,1,128]{2,1,0:T(1,128)} %bitcast.75), calls=%async_computation | async-start | bytes 131072 | tf_op jit(solution)/shard_map/while/body/eval_jaxpr/all_to_all | solution.py:467
  229.4 9.1 %collective-permute-start.2 = (f32[24,128]{1,0:T(8,128)S(1)}, f32[24,128]{1,0:T(8,128)S(1)}, u32[]{:S(2)}, u32[]{:S(2)}) collective-permute-start(f32[24,128]{1,0:T(8,128)S(1)} %get-tuple-element.545), channel_id=1, source_target_pairs={{0,1},{1,2},{2,3},{3,0},{4,5},{5,6},{6,7},{7,4},{8,9},{9,10},{10,1... | collective-permute-start | bytes 36872 | tf_op jit(solution)/shard_map/while/body/eval_jaxpr/ppermute | solution.py:470
  245.1 18.5 %all-to-all-start = ((f32[128,1,128]{2,1,0:T(1,128)}), f32[128,1,128]{2,1,0:T(1,128)S(1)}, u32[]{:S(2)}, u32[]{:S(2)}) async-start(f32[128,1,128]{2,1,0:T(1,128)} %bitcast.75), calls=%async_computation | async-start | bytes 131072 | tf_op jit(solution)/shard_map/while/body/eval_jaxpr/all_to_all | solution.py:467
  253.8 9.1 %collective-permute-start.2 = (f32[24,128]{1,0:T(8,128)S(1)}, f32[24,128]{1,0:T(8,128)S(1)}, u32[]{:S(2)}, u32[]{:S(2)}) collective-permute-start(f32[24,128]{1,0:T(8,128)S(1)} %get-tuple-element.545), channel_id=1, source_target_pairs={{0,1},{1,2},{2,3},{3,0},{4,5},{5,6},{6,7},{7,4},{8,9},{9,10},{10,1... | collective-permute-start | bytes 36872 | tf_op jit(solution)/shard_map/while/body/eval_jaxpr/ppermute | solution.py:470
  269.5 18.5 %all-to-all-start = ((f32[128,1,128]{2,1,0:T(1,128)}), f32[128,1,128]{2,1,0:T(1,128)S(1)}, u32[]{:S(2)}, u32[]{:S(2)}) async-start(f32[128,1,128]{2,1,0:T(1,128)} %bitcast.75), calls=%async_computation | async-start | bytes 131072 | tf_op jit(solution)/shard_map/while/body/eval_jaxpr/all_to_all | solution.py:467
  293.8 18.5 %all-to-all-start = ((f32[128,1,128]{2,1,0:T(1,128)}), f32[128,1,128]{2,1,0:T(1,128)S(1)}, u32[]{:S(2)}, u32[]{:S(2)}) async-start(f32[128,1,128]{2,1,0:T(1,128)} %bitcast.75), calls=%async_computation | async-start | bytes 131072 | tf_op jit(solution)/shard_map/while/body/eval_jaxpr/all_to_all | solution.py:467
  318.2 18.5 %all-to-all-start = ((f32[128,1,128]{2,1,0:T(1,128)}), f32[128,1,128]{2,1,0:T(1,128)S(1)}, u32[]{:S(2)}, u32[]{:S(2)}) async-start(f32[128,1,128]{2,1,0:T(1,128)} %bitcast.75), calls=%async_computation | async-start | bytes 131072 | tf_op jit(solution)/shard_map/while/body/eval_jaxpr/all_to_all | solution.py:467
  342.5 18.5 %all-to-all-start = ((f32[128,1,128]{2,1,0:T(1,128)}), f32[128,1,128]{2,1,0:T(1,128)S(1)}, u32[]{:S(2)}, u32[]{:S(2)}) async-start(f32[128,1,128]{2,1,0:T(1,128)} %bitcast.75), calls=%async_computation | async-start | bytes 131072 | tf_op jit(solution)/shard_map/while/body/eval_jaxpr/all_to_all | solution.py:467
  366.9 18.5 %all-to-all-start = ((f32[128,1,128]{2,1,0:T(1,128)}), f32[128,1,128]{2,1,0:T(1,128)S(1)}, u32[]{:S(2)}, u32[]{:S(2)}) async-start(f32[128,1,128]{2,1,0:T(1,128)} %bitcast.75), calls=%async_computation | async-start | bytes 131072 | tf_op jit(solution)/shard_map/while/body/eval_jaxpr/all_to_all | solution.py:467
  (63 other events, 532.7 us)
